TPU v7x, 256 devices: a whole 4x4x8 slice. The times are simulated.
256 devices in a mesh: dp: 16 (over y, x_lo, core), mp: 16 (over x_hi, z).
Axes of the slice: x: 4 (x_hi: 2, x_lo: 2; x = x_hi * 2 + x_lo), y: 4, z: 8, core: 2. Of those that a mesh axis runs over, the one named last changes fastest.
Arguments:
- token_ids: int32 [32, 16], replicated, may hold values from 0 to 64511
- prompt_lengths: int32 [32], replicated, may hold values from 128 to 6144, as said below
- cache_codes: bfloat16 [32, 6144, 2, 1024], P('dp', 'mp'), may hold values from -1 to 1
- cache_scales: bfloat16 [32, 48, 2, 1024], P('dp', 'mp'), may hold values from 0.03 to 400
- embedding: bfloat16 [64512, 8192], P('mp', 'dp'), may hold values from -12 to 12
- norm_gain: bfloat16 [8192], P('dp'), may hold values from 0.099609375 to 1.8984375
- query_weight: bfloat16 [8192, 8192], P('dp', 'mp'), may hold values from -0.0625 to 0.0625
- key_value_weight: bfloat16 [8192, 2, 1024], P('dp'), may hold values from -0.0625 to 0.0625
- output_weight: bfloat16 [8192, 8192], P('mp', 'dp'), may hold values from -0.0625 to 0.0625
Outputs:
- layer_out: bfloat16 [32, 16, 8192], P(None, None, 'dp')
Inputs may be any that keep to these rules, and one draw needn't show every extreme that they name: `prompt_lengths`: each a multiple of 128; some row has exactly 6144 in every draw.
All inputs are finite; a program needn't handle non-finite values.
Results may differ from a plain program's by a relative error of at most 0.0065.
The roundings to bfloat16 on the way count: a program that leaves them out, or rounds other values in their place, can miss the bound.
Values may be sent and summed in bfloat16 or wider, within the bound.
A program may use at most 128 MiB of HBM per device.

v0:
```python
import math
import jax
import jax.numpy as jnp
from jax import lax
from jax.sharding import PartitionSpec as P

D = 8192
QH = 64
KVH = 8
HEAD = 128
FACTOR_GROUP = 128
NEW = 16
ROPE_BASE = 500000.0
EPSILON = 1e-05
LOWEST = -1e30


def split_up(shard, dim, devices):
    before, after = (shard.shape[:dim], shard.shape[dim + 1 :])
    return jnp.moveaxis(shard.reshape(*before, devices, -1, *after), dim, 0)


def sent_and_summed(shard, axis, dim):
    pieces = split_up(shard, dim, lax.axis_size(axis))
    arrived = lax.all_to_all(pieces, axis, split_axis=0, concat_axis=0, tiled=True)
    return arrived.sum(axis=0)


def rows_for(lines, devices):
    spare = -len(lines) % devices
    return jnp.pad(lines, [(0, spare)] + [(0, 0)] * (lines.ndim - 1))


def joined_along(pieces, dim):
    shape = list(pieces.shape[1:])
    shape[dim] *= pieces.shape[0]
    return jnp.moveaxis(pieces, 0, dim).reshape(shape)


def copy_for_each(shard, axis):
    copies = jnp.broadcast_to(shard, (lax.axis_size(axis), *shard.shape))
    return lax.all_to_all(copies, axis, split_axis=0, concat_axis=0, tiled=True)


def gather_directly(shard, axis, dim):
    return joined_along(copy_for_each(shard, axis), dim)


def total_of(shard, axes):
    lines = shard.reshape(-1, shard.shape[-1])
    own = sent_and_summed(rows_for(lines, lax.axis_size(axes)), axes, 0)
    whole = gather_directly(own, axes, 0)
    return whole[: len(lines)].reshape(shard.shape)


def sent_together(arrays, axis, dim, along):
    ends, at = ([], 0)
    for a in arrays[:-1]:
        at += a.shape[along]
        ends.append(at)
    both = jnp.concatenate(arrays, axis=along)
    return tuple(jnp.split(lax.all_gather(both, axis, axis=dim, tiled=True), ends, axis=along))


def collected_together(shard, axis):
    leaves = jax.tree.leaves(shard)
    order = sorted(range(len(leaves)), key=lambda k: -leaves[k].size)
    width = (1, *leaves[order[0]].shape)[-1]
    lines = [
        jnp.pad(leaves[k].reshape(-1), (0, -leaves[k].size % width)).reshape(-1, width)
        for k in order
    ]
    both, at, found = (copy_for_each(jnp.concatenate(lines), axis), 0, {})
    for k, line in zip(order, lines):
        share = both[:, at : at + len(line)].reshape(len(both), -1)
        found[k] = share[:, : leaves[k].size].reshape(-1, *leaves[k].shape)
        at += len(line)
    numbers = iter(range(len(leaves)))
    return jax.tree.map(lambda _: found[next(numbers)], shard)


def combined_pairwise(pieces, combine):
    while len(jax.tree.leaves(pieces)[0]) > 1:
        pieces = jax.vmap(combine)(
            *(jax.tree.map(lambda part: part[side::2], pieces) for side in (0, 1))
        )
    return jax.tree.map(lambda part: part[0], pieces)


def joined_all(shard, axis, combine):
    pieces = collected_together(shard, axis)
    return combined_pairwise(pieces, combine)


def sent_together_2(arrays, axis, dim, along):
    widths = [math.prod(a.shape[along:]) for a in arrays]
    both = jnp.concatenate(
        [a.reshape(*a.shape[:along], w) for a, w in zip(arrays, widths)], axis=along
    )
    whole = lax.psum_scatter(both, axis, scatter_dimension=dim, tiled=True)
    pieces = jnp.split(whole, [sum(widths[:k]) for k in range(1, len(widths))], axis=along)
    return tuple(
        (b.reshape(*whole.shape[:along], *a.shape[along:]) for a, b in zip(arrays, pieces))
    )


def rotate(values, positions):
    width = values.shape[-1]
    half_width = width // 2
    exponent = jnp.arange(half_width, dtype=jnp.float32) * (2.0 / width)
    rates = jnp.exp(-jnp.log(ROPE_BASE) * exponent)
    angles = positions[..., None].astype(jnp.float32) * rates
    cosine = jnp.cos(angles)
    sinus_term = jnp.sin(angles)
    first = values[..., :half_width]
    second = values[..., half_width:]
    return jnp.concatenate(
        [first * cosine - second * sinus_term, second * cosine + first * sinus_term], axis=-1
    )


def tensor_total(partial_value):
    return total_of(partial_value, "mp")


def combine_totals(earlier, later):
    largest = jnp.maximum(earlier[0], later[0])
    return (
        largest,
        earlier[1] * jnp.exp(earlier[0] - largest) + later[1] * jnp.exp(later[0] - largest),
    )


def attend_in_place(queries, new_keys, new_values, cache_codes, cache_scales, lengths, place):
    rows_local = queries.shape[0]
    whole_queries, whole_keys, whole_values = (
        lax.all_gather(queries, "mp", axis=2, tiled=True),
        *sent_together((new_keys, new_values), "mp", 2, 0),
    )
    pair = whole_keys.shape[2] // KVH
    whole_keys = whole_keys.reshape(rows_local, NEW, KVH, pair, HEAD)[:, :, :, 0]
    whole_values = whole_values.reshape(rows_local, NEW, KVH, pair, HEAD)[:, :, :, 0]
    grouped = whole_queries.reshape(rows_local, NEW, KVH, QH // KVH, HEAD)
    span = cache_codes.shape[1]
    widened = cache_codes.astype(jnp.float32).reshape(
        rows_local, span // FACTOR_GROUP, FACTOR_GROUP, 2, KVH * HEAD
    )
    block_scales = cache_scales.astype(jnp.float32).reshape(
        rows_local, span // FACTOR_GROUP, 1, 2, KVH * HEAD
    )
    cache = (widened * block_scales).astype(jnp.bfloat16).reshape(rows_local, span, 2, KVH, HEAD)
    factor = HEAD ** (-0.5)
    older = (
        jnp.einsum("rtkgd,rskd->rkgts", grouped, cache[:, :, 0], preferred_element_type=jnp.float32)
        * factor
    )
    fresh = (
        jnp.einsum("rtkgd,rukd->rkgtu", grouped, whole_keys, preferred_element_type=jnp.float32)
        * factor
    )
    slots = place * span + jnp.arange(span, dtype=jnp.int32)
    older_allowed = (slots[None, :] < lengths[:, None])[:, None, None, None, :]
    steps = jnp.arange(NEW, dtype=jnp.int32)
    fresh_allowed = (steps[None, :] <= steps[:, None]) & (place == 0)
    older = jnp.where(older_allowed, older, -jnp.inf)
    fresh = jnp.where(fresh_allowed, fresh, -jnp.inf)
    top = jnp.maximum(jnp.maximum(jnp.max(older, axis=-1), jnp.max(fresh, axis=-1)), LOWEST)[
        ..., None
    ]
    total = jnp.sum(jnp.exp(older - top), axis=-1, keepdims=True) + jnp.sum(
        jnp.exp(fresh - top), axis=-1, keepdims=True
    )
    largest, whole_total = joined_all((top, total), "mp", combine_totals)
    older_weights = (jnp.exp(older - largest) / whole_total).astype(jnp.bfloat16)
    fresh_weights = (jnp.exp(fresh - largest) / whole_total).astype(jnp.bfloat16)
    partial_value = jnp.einsum(
        "rkgts,rskd->rtkgd", older_weights, cache[:, :, 1], preferred_element_type=jnp.float32
    )
    partial_value = partial_value + jnp.einsum(
        "rkgtu,rukd->rtkgd", fresh_weights, whole_values, preferred_element_type=jnp.float32
    )
    partial_value = partial_value.reshape(rows_local, NEW, QH, HEAD)
    summed = sent_and_summed(partial_value, "mp", 2)
    return summed.astype(jnp.bfloat16)


def on_device(
    token_ids,
    prompt_lengths,
    cache_codes,
    cache_scales,
    embedding,
    norm_gain,
    query_weight,
    key_value_weight,
    output_weight,
):
    parts = lax.axis_size("mp")
    place = lax.axis_index("mp")
    batch_index = lax.axis_index("dp")
    pair = max(parts // KVH, 1)
    per_device = max(KVH // parts, 1)
    rows_local = cache_codes.shape[0]
    vocab_local = embedding.shape[0]
    local_heads = query_weight.shape[1] // HEAD
    local_ids = token_ids.reshape(-1) - place * vocab_local
    inside = (local_ids >= 0) & (local_ids < vocab_local)
    picked = jnp.take(embedding, jnp.clip(local_ids, 0, vocab_local - 1), axis=0)
    embedded = tensor_total(jnp.where(inside[:, None], picked.astype(jnp.float32), 0.0))
    scaled = (embedded * norm_gain.astype(jnp.float32)).astype(jnp.bfloat16)
    squares = jnp.sum(embedded * embedded, axis=1)
    first_head = place // pair * per_device
    weight_slice = lax.dynamic_slice_in_dim(
        key_value_weight, first_head * HEAD, per_device * HEAD, axis=2
    )
    weight_slice = weight_slice.reshape(weight_slice.shape[0], 2 * per_device * HEAD)
    query_part = jnp.dot(scaled, query_weight, preferred_element_type=jnp.float32)
    fresh_part = jnp.dot(scaled, weight_slice, preferred_element_type=jnp.float32)
    query_sum, fresh_sum, square_sum = sent_together_2(
        (query_part, fresh_part, squares), "dp", 0, 1
    )
    inverse = lax.rsqrt(square_sum / D + EPSILON)[:, None]
    lengths = lax.dynamic_slice_in_dim(prompt_lengths, batch_index * rows_local, rows_local)
    positions = (lengths[:, None] + jnp.arange(NEW, dtype=jnp.int32)[None, :])[:, :, None]
    queries = rotate(
        (query_sum * inverse).reshape(rows_local, NEW, local_heads, HEAD), positions
    ).astype(jnp.bfloat16)
    fresh = (fresh_sum * inverse).reshape(rows_local, NEW, 2, per_device, HEAD)
    new_keys = rotate(fresh[:, :, 0], positions).astype(jnp.bfloat16)
    new_values = fresh[:, :, 1].astype(jnp.bfloat16)
    mixed = attend_in_place(
        queries, new_keys, new_values, cache_codes, cache_scales, lengths, place
    )
    mixed = mixed.reshape(rows_local * NEW, local_heads * HEAD)
    partial_value = jnp.dot(
        gather_directly(mixed, "dp", 0), output_weight, preferred_element_type=jnp.float32
    )
    result = tensor_total(partial_value).astype(jnp.bfloat16)
    return result.reshape(token_ids.shape[0], token_ids.shape[1], output_weight.shape[1])


def solution(mesh):
    return jax.shard_map(
        on_device,
        mesh=mesh,
        in_specs=(
            P(),
            P(),
            P("dp", "mp", None, None),
            P("dp", "mp", None, None),
            P("mp", "dp"),
            P("dp"),
            P("dp", "mp"),
            P("dp", None, None),
            P("mp", "dp"),
        ),
        out_specs=P(None, None, "dp"),
        check_vma=False,
    )
```

profile of v0, /device:TPU:2, one launch (start us, length us, event | category | flops | bytes accessed | tf_op | source)
XLA Modules:
  0.0 366.9 jit_solution(13847323160019481383)
XLA Ops:
  8.5 4.7 %gather_fusion = bf16[512,512]{1,0:T(8,128)(2,1)S(1)} fusion(bf16[4032,512]{1,0:T(8,128)(2,1)} %param.13, s32[1024]{0:T(1024)S(1)} %pad_clamp_fusion), kind=kCustom, calls=%fused_computation | custom fusion | bytes 1050624 | tf_op jit(solution)/shard_map/jit(_take)/gather | solution.py:208
  13.5 38.3 %all_to_all.35 = f32[16,32,512]{2,1,0:T(8,128)S(1)} all-to-all(f32[16,32,512]{2,1,0:T(8,128)S(1)} %convert_select_fusion), channel_id=1, replica_groups=mesh['dp'=16,'mp'=16] {'mp'}, dimensions={0} | all-to-all | bytes 2097152 | tf_op jit(solution)/shard_map/all_to_all | solution.py:25
  51.9 1.1 broadcast_in_dim.74
  53.0 4.6 %all-to-all-start.1 = ((f32[16,32,512]{2,1,0:T(8,128)}), f32[16,32,512]{2,1,0:T(8,128)S(1)}, u32[]{:S(2)}, u32[]{:S(2)}) async-start(f32[16,32,512]{2,1,0:T(8,128)} %broadcast_in_dim.74), calls=%async_computation.1 | async-start | bytes 2097152 | tf_op jit(solution)/shard_map/all_to_all | solution.py:42
  57.9 27.4 %all-to-all-done.1 = f32[16,32,512]{2,1,0:T(8,128)S(1)} async-done(((f32[16,32,512]{2,1,0:T(8,128)}), f32[16,32,512]{2,1,0:T(8,128)S(1)}, u32[]{:S(2)}, u32[]{:S(2)}) %all-to-all-start.1) | async-done | bytes 1048608 | tf_op jit(solution)/shard_map/all_to_all | solution.py:42
  86.7 1.7 copy.140
  89.2 4.2 %copy.151 = f32[192,8,8,128]{3,2,1,0:T(8,128)} copy(f32[192,8,8,128]{3,1,2,0:T(8,128)S(1)} %bitcast.116) | data formatting | bytes 12582912
  93.4 8.8 %copy.112 = bf16[2,384,2,1024]{1,3,2,0:T(8,128)(2,1)} copy(bf16[2,384,2,1024]{3,2,1,0:T(2,128)(2,1)} %param.11) | data formatting | bytes 6291456 | tf_op args[2]
  102.2 5.4 %copy.114 = f32[2,384,2,8,128]{4,1,3,0,2:T(8,128)} copy(bf16[2,384,2,8,128]{1,4,3,2,0:T(8,128)(2,1)} %bitcast.118) | data formatting | bytes 9437184 | tf_op jit(solution)/shard_map/reshape | solution.py:145
  108.0 7.9 %fusion = bf16[2,384,2,8,128]{4,1,3,0,2:T(8,128)(2,1)} fusion(f32[2,384,2,8,128]{4,1,3,0,2:T(8,128)} %copy.114, f32[2,384,2,8,128]{4,3,1,2,0:T(8,128)} %bitcast.117), kind=kLoop, calls=%fused_computation.2 | loop fusion | flops 3145728 | bytes 15728640 | tf_op jit(solution)/shard_map/convert_element_type | solution.py:151
  115.9 33.1 %reduce-scatter.4.cloned.1.call-done = f32[32,769]{1,0:T(8,128)} async-done(((f32[512,769]{1,0:T(8,128)}), f32[32,769]{1,0:T(8,128)}) %reduce-scatter.4.cloned.1.call-update) | async-done | bytes 98448 | tf_op jit(solution)/shard_map/reduce_scatter | solution.py:100
  150.9 42.0 %all_gather.7 = bf16[4,16,16,128]{3,1,0,2:T(8,128)(2,1)S(1)} all-gather(bf16[4,16,1,128]{3,1,0,2:T(8,128)(2,1)S(1)} %pad_maximum_fusion.2), channel_id=1, replica_groups=mesh['dp'=16,'mp'=16] {'mp'}, dimensions={2}, use_global_device_ids=true | all-gather | bytes 278528 | tf_op jit(solution)/shard_map/all_gather | solution.py:62
  194.1 38.7 %all_gather.6 = bf16[2,16,64,128]{3,1,0,2:T(8,128)(2,1)S(1)} all-gather(bf16[2,16,4,128]{3,1,0,2:T(8,128)(2,1)S(1)} %copy.120), channel_id=1, replica_groups=mesh['dp'=16,'mp'=16] {'mp'}, dimensions={2}, use_global_device_ids=true | all-gather | bytes 557056 | tf_op jit(solution)/shard_map/all_gather | solution.py:137
  232.8 1.4 fusion.34
  234.2 2.5 bitcast_reduce_fusion
  237.1 2.8 fusion.2
  241.0 4.3 %all-to-all-start.2 = ((f32[16,4096,1]{1,2,0:T(1,128)}), f32[16,4096,1]{1,2,0:T(1,128)S(1)}, u32[]{:S(2)}, u32[]{:S(2)}) async-start(f32[16,4096,1]{1,2,0:T(1,128)} %broadcast_in_dim.78), calls=%async_computation.2 | async-start | bytes 524288 | tf_op jit(solution)/shard_map/all_to_all | solution.py:42
  245.3 11.1 %all-to-all-done.2 = f32[16,4096,1]{1,2,0:T(1,128)S(1)} async-done(((f32[16,4096,1]{1,2,0:T(1,128)}), f32[16,4096,1]{1,2,0:T(1,128)S(1)}, u32[]{:S(2)}, u32[]{:S(2)}) %all-to-all-start.2) | async-done | bytes 262176 | tf_op jit(solution)/shard_map/all_to_all | solution.py:42
  258.3 1.5 copy-done.2
  259.8 2.2 fusion.7
  262.5 24.7 %all_to_all.36 = f32[16,2,16,4,128]{4,2,3,1,0:T(8,128)S(1)} all-to-all(f32[16,2,16,4,128]{4,2,3,1,0:T(8,128)S(1)} %bitcast.121), channel_id=1, replica_groups=mesh['dp'=16,'mp'=16] {'mp'}, dimensions={0} | all-to-all | bytes 2097152 | tf_op jit(solution)/shard_map/all_to_all | solution.py:25
  287.3 17.1 %all_to_all.37 = bf16[16,32,512]{2,1,0:T(8,128)(2,1)S(1)} all-to-all(bf16[16,32,512]{2,1,0:T(8,128)(2,1)S(1)} %broadcast_in_dim.79), channel_id=1, replica_groups=mesh['dp'=16,'mp'=16] {'dp'}, dimensions={0} | all-to-all | bytes 1048576 | tf_op jit(solution)/shard_map/all_to_all | solution.py:42
  304.9 32.5 %all_to_all.38 = f32[16,32,512]{2,1,0:T(8,128)S(1)} all-to-all(f32[16,32,512]{2,1,0:T(8,128)S(1)} %fusion.13), channel_id=1, replica_groups=mesh['dp'=16,'mp'=16] {'mp'}, dimensions={0} | all-to-all | bytes 2097152 | tf_op jit(solution)/shard_map/all_to_all | solution.py:25
  337.5 21.8 %all_to_all.39 = bf16[16,32,512]{2,1,0:T(8,128)(2,1)S(1)} all-to-all(bf16[16,32,512]{2,1,0:T(8,128)(2,1)S(1)} %broadcast_in_dim.80), channel_id=1, replica_groups=mesh['dp'=16,'mp'=16] {'mp'}, dimensions={0} | all-to-all | bytes 1048576 | tf_op jit(solution)/shard_map/all_to_all | solution.py:42
  (90 shorter events, 13.4 us)
Async XLA Ops:
  6.5 51.1 %copy-start = (bf16[512,2,1024]{2,1,0:T(2,128)(2,1)S(1)}, bf16[512,2,1024]{2,1,0:T(2,128)(2,1)}, u32[]{:S(2)}) copy-start(bf16[512,2,1024]{2,1,0:T(2,128)(2,1)} %param.16) | copy-start | bytes 6291460
  13.4 44.2 %copy-start.7 = (bf16[512]{0:T(512)(128)(2,1)S(1)}, bf16[512]{0:T(512)(128)(2,1)}, u32[]{:S(2)}) copy-start(bf16[512]{0:T(512)(128)(2,1)} %param.14) | copy-start | bytes 3076
  53.0 32.3 %all-to-all-start.1 = ((f32[16,32,512]{2,1,0:T(8,128)}), f32[16,32,512]{2,1,0:T(8,128)S(1)}, u32[]{:S(2)}, u32[]{:S(2)}) async-start(f32[16,32,512]{2,1,0:T(8,128)} %broadcast_in_dim.74), calls=%async_computation.1 | async-start | bytes 2097152 | tf_op jit(solution)/shard_map/all_to_all | solution.py:42
  57.6 91.4 %reduce-scatter.4.cloned.1.call-start = ((), (), s32[]{:S(2)}) async-start(), calls=%async_computation.8 | async-start | bytes 1949696 | tf_op jit(solution)/shard_map/reduce_scatter | solution.py:100
  57.9 28.2 %copy-start.4 = (bf16[512,512]{1,0:T(8,128)(2,1)S(1)}, bf16[512,512]{1,0:T(8,128)(2,1)}, u32[]{:S(2)}) copy-start(bf16[512,512]{1,0:T(8,128)(2,1)} %param.15) | copy-start | bytes 1572868
  86.7 1.7 copy-start.6
  102.2 5.4 %copy-start.8 = (s32[32]{0:T(128)S(1)}, s32[32]{0:T(128)}, u32[]{:S(2)}) copy-start(s32[32]{0:T(128)} %param.10) | copy-start | bytes 388
  193.9 40.3 %copy-start.3 = (bf16[2,384,2,8,128]{4,1,3,0,2:T(8,128)(2,1)S(1)}, bf16[2,384,2,8,128]{4,1,3,0,2:T(8,128)(2,1)}, u32[]{:S(2)}) copy-start(bf16[2,384,2,8,128]{4,1,3,0,2:T(8,128)(2,1)} %fusion) | copy-start | bytes 9437188
  241.0 15.5 %all-to-all-start.2 = ((f32[16,4096,1]{1,2,0:T(1,128)}), f32[16,4096,1]{1,2,0:T(1,128)S(1)}, u32[]{:S(2)}, u32[]{:S(2)}) async-start(f32[16,4096,1]{1,2,0:T(1,128)} %broadcast_in_dim.78), calls=%async_computation.2 | async-start | bytes 524288 | tf_op jit(solution)/shard_map/all_to_all | solution.py:42
  257.9 1.9 copy-start.2
  262.4 42.0 %copy-start.5 = (bf16[512,512]{1,0:T(8,128)(2,1)S(1)}, bf16[512,512]{1,0:T(8,128)(2,1)}, u32[]{:S(2)}) copy-start(bf16[512,512]{1,0:T(8,128)(2,1)} %param.17) | copy-start | bytes 1572868
  304.5 55.6 %copy-start.1 = (bf16[512,2,1024]{2,1,0:T(2,128)(2,1)S(1)}, bf16[512,2,1024]{2,1,0:T(2,128)(2,1)}, u32[]{:S(2)}) copy-start(bf16[512,2,1024]{2,1,0:T(2,128)(2,1)} %param.16) | copy-start | bytes 6291460
Sparse Core Ops, SparseCore 0:
  88.5 60.4 reduce-scatter.3
where the time goes:
time: 368 us; the launch traced here: 367 us
  blocking collectives  215 us (58%)
  waiting for transfers between devices  71.7 us (19%)
  local copies, waits for them, and re-layouts  32.6 us (9%)
  other arithmetic  17.1 us (5%)
  between operations  13.9 us (4%)
  starting transfers between devices  8.95 us (2%)
  matrix products  7.7 us (2%)
    all_to_all x3, blocking collectives, sent_and_summed(): lax.all_to_all(pieces, axis, split_axis=0, concat_axis=0, tiled=True)  95.5 us
    all_gather x1, blocking collectives, sent_together(): lax.all_gather(both, axis, axis=dim, tiled=True)  42 us
    all_to_all x2, blocking collectives, copy_for_each(): return lax.all_to_all(copies, axis, split_axis=0, concat_axis=0, tiled=True)  38.9 us
    all_gather x1, blocking collectives, attend_in_place(): lax.all_gather(queries, 'mp', axis=2, tiled=True)  38.7 us
    all_to_all x2, waiting for transfers between devices, copy_for_each(): return lax.all_to_all(copies, axis, split_axis=0, concat_axis=0, tiled=True)  38.6 us
    reduce_scatter x1, waiting for transfers between devices, sent_together_2(): whole = lax.psum_scatter(both, axis, scatter_dimension=dim, tiled=True)  33.1 us
    unnamed x27, local copies, waits for them, and re-layouts  17.1 us
    all_to_all x2, starting transfers between devices, copy_for_each(): return lax.all_to_all(copies, axis, split_axis=0, concat_axis=0, tiled=True)  8.9 us
  transfers between devices with their start and end apart: 3, of which 3 were waited for; matrix products, arithmetic and copies ran while one was open for 8% of the time, Pallas kernels for 0%

commit v1 on v0

--- a/solution.py
+++ b/solution.py
@@ -134,7 +134,9 @@
 def attend_in_place(queries, new_keys, new_values, cache_codes, cache_scales, lengths, place):
     rows_local = queries.shape[0]
     whole_queries, whole_keys, whole_values = (
-        lax.all_gather(queries, "mp", axis=2, tiled=True),
+        jnp.concatenate(
+            lax.all_to_all(jnp.stack([queries] * lax.axis_size("mp")), "mp", 0, 0), axis=2
+        ),
         *sent_together((new_keys, new_values), "mp", 2, 0),
     )
     pair = whole_keys.shape[2] // KVH

time: 368 us -> 344 us (0.935)
  blocking collectives: 215 us -> 182 us
  starting transfers between devices: 8.95 us -> 16.8 us
    all_gather x1 -> x0, blocking collectives: 38.7 us -> none  [attend_in_place(): lax.all_gather(queries, 'mp', axis=2, tiled=True)]
    all_to_all x0 -> x1, starting transfers between devices: none -> 8.6 us  [attend_in_place(): lax.all_to_all(jnp.stack([queries] * lax.axis_size('mp')), 'mp', 0, 0)]
    all_to_all x2, blocking collectives: 38.9 us -> 43.1 us  [copy_for_each(): return lax.all_to_all(copies, axis, split_axis=0, concat_axis=0, tiled=True)]
    unnamed x27 -> x25, local copies, waits for them, and re-layouts: 17.1 us -> 17.1 us
  transfers between devices with their start and end apart: 3 -> 4, of which waited for: 3 -> 3; matrix products, arithmetic and copies ran while one was open for 8% -> 8% of each run, Pallas kernels for 0% -> 0%
where the time goes in v1:
time: 344 us; the launch traced here: 343 us
  blocking collectives  182 us (53%)
  waiting for transfers between devices  70.9 us (21%)
  local copies, waits for them, and re-layouts  33.5 us (10%)
  other arithmetic  17.1 us (5%)
  starting transfers between devices  16.8 us (5%)
  between operations  13.9 us (4%)
  matrix products  9.09 us (3%)
    all_to_all x3, blocking collectives, sent_and_summed(): lax.all_to_all(pieces, axis, split_axis=0, concat_axis=0, tiled=True)  95 us
    all_gather x1, blocking collectives, sent_together(): lax.all_gather(both, axis, axis=dim, tiled=True)  43.6 us
    all_to_all x2, blocking collectives, copy_for_each(): return lax.all_to_all(copies, axis, split_axis=0, concat_axis=0, tiled=True)  43.1 us
    all_to_all x2, waiting for transfers between devices, copy_for_each(): return lax.all_to_all(copies, axis, split_axis=0, concat_axis=0, tiled=True)  37.8 us
    reduce_scatter x1, waiting for transfers between devices, sent_together_2(): whole = lax.psum_scatter(both, axis, scatter_dimension=dim, tiled=True)  33.1 us
    unnamed x25, local copies, waits for them, and re-layouts  17.1 us
    all_to_all x1, starting transfers between devices, attend_in_place(): lax.all_to_all(jnp.stack([queries] * lax.axis_size('mp')), 'mp', 0, 0)  8.6 us
    all_to_all x2, starting transfers between devices, copy_for_each(): return lax.all_to_all(copies, axis, split_axis=0, concat_axis=0, tiled=True)  8.11 us
  transfers between devices with their start and end apart: 4, of which 3 were waited for; matrix products, arithmetic and copies ran while one was open for 8% of the time, Pallas kernels for 0%

profile of v1, /device:TPU:2, one launch (start us, length us, event | category | flops | bytes accessed | tf_op | source)
XLA Modules:
  0.0 342.9 jit_solution(2878115428056862522)
XLA Ops:
  8.5 4.7 %gather_fusion = bf16[512,512]{1,0:T(8,128)(2,1)S(1)} fusion(bf16[4032,512]{1,0:T(8,128)(2,1)} %param.13, s32[1024]{0:T(1024)S(1)} %pad_clamp_fusion), kind=kCustom, calls=%fused_computation | custom fusion | bytes 1050624 | tf_op jit(solution)/shard_map/jit(_take)/gather | solution.py:210
  13.5 38.3 %all_to_all.40 = f32[16,32,512]{2,1,0:T(8,128)S(1)} all-to-all(f32[16,32,512]{2,1,0:T(8,128)S(1)} %convert_select_fusion), channel_id=1, replica_groups=mesh['dp'=16,'mp'=16] {'mp'}, dimensions={0} | all-to-all | bytes 2097152 | tf_op jit(solution)/shard_map/all_to_all | solution.py:25
  51.9 1.1 broadcast_in_dim.74
  53.0 4.6 %all-to-all-start.1 = ((f32[16,32,512]{2,1,0:T(8,128)}), f32[16,32,512]{2,1,0:T(8,128)S(1)}, u32[]{:S(2)}, u32[]{:S(2)}) async-start(f32[16,32,512]{2,1,0:T(8,128)} %broadcast_in_dim.74), calls=%async_computation.1 | async-start | bytes 2097152 | tf_op jit(solution)/shard_map/all_to_all | solution.py:42
  57.9 27.4 %all-to-all-done.1 = f32[16,32,512]{2,1,0:T(8,128)S(1)} async-done(((f32[16,32,512]{2,1,0:T(8,128)}), f32[16,32,512]{2,1,0:T(8,128)S(1)}, u32[]{:S(2)}, u32[]{:S(2)}) %all-to-all-start.1) | async-done | bytes 1048608 | tf_op jit(solution)/shard_map/all_to_all | solution.py:42
  86.7 1.7 copy.140
  89.2 4.2 %copy.151 = f32[192,8,8,128]{3,2,1,0:T(8,128)} copy(f32[192,8,8,128]{3,1,2,0:T(8,128)S(1)} %bitcast.127) | data formatting | bytes 12582912
  93.4 8.8 %copy.112 = bf16[2,384,2,1024]{1,3,2,0:T(8,128)(2,1)} copy(bf16[2,384,2,1024]{3,2,1,0:T(2,128)(2,1)} %param.11) | data formatting | bytes 6291456 | tf_op args[2]
  102.2 5.4 %copy.114 = f32[2,384,2,8,128]{4,1,3,0,2:T(8,128)} copy(bf16[2,384,2,8,128]{1,4,3,2,0:T(8,128)(2,1)} %bitcast.129) | data formatting | bytes 9437184 | tf_op jit(solution)/shard_map/reshape | solution.py:147
  108.0 7.9 %fusion = bf16[2,384,2,8,128]{4,1,3,0,2:T(8,128)(2,1)} fusion(f32[2,384,2,8,128]{4,1,3,0,2:T(8,128)} %copy.114, f32[2,384,2,8,128]{4,3,1,2,0:T(8,128)} %bitcast.128), kind=kLoop, calls=%fused_computation.2 | loop fusion | flops 3145728 | bytes 15728640 | tf_op jit(solution)/shard_map/convert_element_type | solution.py:153
  115.9 33.1 %reduce-scatter.4.cloned.1.call-done = f32[32,769]{1,0:T(8,128)} async-done(((f32[512,769]{1,0:T(8,128)}), f32[32,769]{1,0:T(8,128)}) %reduce-scatter.4.cloned.1.call-update) | async-done | bytes 98448 | tf_op jit(solution)/shard_map/reduce_scatter | solution.py:100
  151.9 8.6 %all-to-all-start.2 = ((bf16[16,2,16,4,128]{4,2,3,1,0:T(8,128)(2,1)}), bf16[16,2,16,4,128]{4,2,3,1,0:T(8,128)(2,1)S(1)}, u32[]{:S(2)}, u32[]{:S(2)}) async-start(bf16[16,2,16,4,128]{4,2,3,1,0:T(8,128)(2,1)} %stack.2), calls=%async_computation.2 | async-start | bytes 1048576 | tf_op jit(solution)/shard_map/all_to_all | solution.py:138
  161.6 43.6 %all_gather.3 = bf16[4,16,16,128]{3,1,0,2:T(8,128)(2,1)S(1)} all-gather(bf16[4,16,1,128]{3,1,0,2:T(8,128)(2,1)S(1)} %pad_maximum_fusion.2), channel_id=1, replica_groups=mesh['dp'=16,'mp'=16] {'mp'}, dimensions={2}, use_global_device_ids=true | all-gather | bytes 278528 | tf_op jit(solution)/shard_map/all_gather | solution.py:62
  205.3 1.4 fusion.36
  206.7 3.9 %bitcast_reduce_fusion = (f32[2,8,8,16]{3,2,1,0:T(8,128)S(1)}, f32[2,8,384,16,8]{2,3,4,1,0:T(8,128)}) fusion(pred[2,384]{1,0:T(4,128)(4,1)S(1)} %broadcast_compare_fusion, bf16[2,384,2,8,128]{4,1,3,0,2:T(8,128)(2,1)} %fusion, bf16[2,16,8,8,128]{4,1,3,2,0:T(8,128)(2,1)S(1)} %bitcast.131), kind=kOutput, calls=%fused_computation.5 | convolution fusion | flops 203683840 | bytes 5251840 | tf_op jit(solution)/shard_map/rtkgd,rskd->rkgts/dot_general | solution.py:156
  210.9 2.8 fusion.2
  214.8 3.5 %all-to-all-start.3 = ((f32[16,4096,1]{1,2,0:T(1,128)}), f32[16,4096,1]{1,2,0:T(1,128)S(1)}, u32[]{:S(2)}, u32[]{:S(2)}) async-start(f32[16,4096,1]{1,2,0:T(1,128)} %broadcast_in_dim.78), calls=%async_computation.3 | async-start | bytes 524288 | tf_op jit(solution)/shard_map/all_to_all | solution.py:42
  218.4 10.4 %all-to-all-done.3 = f32[16,4096,1]{1,2,0:T(1,128)S(1)} async-done(((f32[16,4096,1]{1,2,0:T(1,128)}), f32[16,4096,1]{1,2,0:T(1,128)S(1)}, u32[]{:S(2)}, u32[]{:S(2)}) %all-to-all-start.3) | async-done | bytes 262176 | tf_op jit(solution)/shard_map/all_to_all | solution.py:42
  230.6 1.5 copy-done.2
  232.0 2.2 fusion.7
  234.8 23.6 %all_to_all.41 = f32[16,2,16,4,128]{4,2,3,1,0:T(8,128)S(1)} all-to-all(f32[16,2,16,4,128]{4,2,3,1,0:T(8,128)S(1)} %bitcast.134), channel_id=1, replica_groups=mesh['dp'=16,'mp'=16] {'mp'}, dimensions={0} | all-to-all | bytes 2097152 | tf_op jit(solution)/shard_map/all_to_all | solution.py:25
  258.6 21.3 %all_to_all.42 = bf16[16,32,512]{2,1,0:T(8,128)(2,1)S(1)} all-to-all(bf16[16,32,512]{2,1,0:T(8,128)(2,1)S(1)} %broadcast_in_dim.79), channel_id=1, replica_groups=mesh['dp'=16,'mp'=16] {'dp'}, dimensions={0} | all-to-all | bytes 1048576 | tf_op jit(solution)/shard_map/all_to_all | solution.py:42
  280.3 33.0 %all_to_all.43 = f32[16,32,512]{2,1,0:T(8,128)S(1)} all-to-all(f32[16,32,512]{2,1,0:T(8,128)S(1)} %fusion.13), channel_id=1, replica_groups=mesh['dp'=16,'mp'=16] {'mp'}, dimensions={0} | all-to-all | bytes 2097152 | tf_op jit(solution)/shard_map/all_to_all | solution.py:25
  313.5 21.8 %all_to_all.44 = bf16[16,32,512]{2,1,0:T(8,128)(2,1)S(1)} all-to-all(bf16[16,32,512]{2,1,0:T(8,128)(2,1)S(1)} %broadcast_in_dim.80), channel_id=1, replica_groups=mesh['dp'=16,'mp'=16] {'mp'}, dimensions={0} | all-to-all | bytes 1048576 | tf_op jit(solution)/shard_map/all_to_all | solution.py:42
  (90 shorter events, 14.3 us)
Async XLA Ops:
  6.5 51.1 %copy-start = (bf16[512,2,1024]{2,1,0:T(2,128)(2,1)S(1)}, bf16[512,2,1024]{2,1,0:T(2,128)(2,1)}, u32[]{:S(2)}) copy-start(bf16[512,2,1024]{2,1,0:T(2,128)(2,1)} %param.16) | copy-start | bytes 6291460
  13.4 44.2 %copy-start.6 = (bf16[512]{0:T(512)(128)(2,1)S(1)}, bf16[512]{0:T(512)(128)(2,1)}, u32[]{:S(2)}) copy-start(bf16[512]{0:T(512)(128)(2,1)} %param.14) | copy-start | bytes 3076
  53.0 32.3 %all-to-all-start.1 = ((f32[16,32,512]{2,1,0:T(8,128)}), f32[16,32,512]{2,1,0:T(8,128)S(1)}, u32[]{:S(2)}, u32[]{:S(2)}) async-start(f32[16,32,512]{2,1,0:T(8,128)} %broadcast_in_dim.74), calls=%async_computation.1 | async-start | bytes 2097152 | tf_op jit(solution)/shard_map/all_to_all | solution.py:42
  57.6 91.4 %reduce-scatter.4.cloned.1.call-start = ((), (), s32[]{:S(2)}) async-start(), calls=%async_computation.9 | async-start | bytes 1949696 | tf_op jit(solution)/shard_map/reduce_scatter | solution.py:100
  57.9 28.2 %copy-start.3 = (bf16[512,512]{1,0:T(8,128)(2,1)S(1)}, bf16[512,512]{1,0:T(8,128)(2,1)}, u32[]{:S(2)}) copy-start(bf16[512,512]{1,0:T(8,128)(2,1)} %param.15) | copy-start | bytes 1572868
  86.7 1.7 copy-start.5
  102.2 5.4 %copy-start.7 = (s32[32]{0:T(128)S(1)}, s32[32]{0:T(128)}, u32[]{:S(2)}) copy-start(s32[32]{0:T(128)} %param.10) | copy-start | bytes 388
  151.9 53.4 %all-to-all-start.2 = ((bf16[16,2,16,4,128]{4,2,3,1,0:T(8,128)(2,1)}), bf16[16,2,16,4,128]{4,2,3,1,0:T(8,128)(2,1)S(1)}, u32[]{:S(2)}, u32[]{:S(2)}) async-start(bf16[16,2,16,4,128]{4,2,3,1,0:T(8,128)(2,1)} %stack.2), calls=%async_computation.2 | async-start | bytes 1048576 | tf_op jit(solution)/shard_map/all_to_all | solution.py:138
  214.8 13.9 %all-to-all-start.3 = ((f32[16,4096,1]{1,2,0:T(1,128)}), f32[16,4096,1]{1,2,0:T(1,128)S(1)}, u32[]{:S(2)}, u32[]{:S(2)}) async-start(f32[16,4096,1]{1,2,0:T(1,128)} %broadcast_in_dim.78), calls=%async_computation.3 | async-start | bytes 524288 | tf_op jit(solution)/shard_map/all_to_all | solution.py:42
  230.1 1.9 copy-start.2
  234.7 45.2 %copy-start.4 = (bf16[512,512]{1,0:T(8,128)(2,1)S(1)}, bf16[512,512]{1,0:T(8,128)(2,1)}, u32[]{:S(2)}) copy-start(bf16[512,512]{1,0:T(8,128)(2,1)} %param.17) | copy-start | bytes 1572868
  279.9 56.2 %copy-start.1 = (bf16[512,2,1024]{2,1,0:T(2,128)(2,1)S(1)}, bf16[512,2,1024]{2,1,0:T(2,128)(2,1)}, u32[]{:S(2)}) copy-start(bf16[512,2,1024]{2,1,0:T(2,128)(2,1)} %param.16) | copy-start | bytes 6291460
Sparse Core Ops, SparseCore 0:
  88.5 60.4 reduce-scatter.3
